TPU v7x, 256 devices: a whole 4x4x8 slice. The times are simulated.
256 devices in a mesh: lat: 2 (over x_hi), lon: 2 (over x_lo), lev: 64 (over z, y, core).
Axes of the slice: x: 4 (x_hi: 2, x_lo: 2; x = x_hi * 2 + x_lo), y: 4, z: 8, core: 2. Of those that a mesh axis runs over, the one named last changes fastest.
Arguments:
- along_axis_flow: bfloat16 [640, 4, 32, 1440], P(('lat', 'lev'), None, None, 'lon'), may hold values from -6 to 6
- poleward_flow: bfloat16 [640, 4, 32, 1440], P(('lat', 'lev'), None, None, 'lon'), may hold values from -6 to 6
- warmth_departure: bfloat16 [640, 4, 32, 1440], P(('lat', 'lev'), None, None, 'lon'), may hold values from -6 to 6
- validity_indicator: int32 [640, 32, 1440], P(('lat', 'lev'), None, 'lon'), may hold values from 0 to 1
- layer_depth_span: float32 [32], replicated, may hold values from 0.3 to 3
- desired_circulation_norm: float32 [640, 4, 32], P(('lat', 'lev')), may hold values from -4 to 4
Outputs:
- psi_norm: float32 [640, 4, 32], P(('lat', 'lev'))
- heat_cospec: float32 [720, 640, 128], P('lon', ('lat', 'lev'))
- momentum_cospec: float32 [720, 640, 128], P('lon', ('lat', 'lev'))
- budget_penalty: float32 [], replicated
All inputs are finite; a program needn't handle non-finite values. Where the computation divides by a largest or mean magnitude, that divisor is 1e-20 or more.
Results may differ from a plain program's by a relative error of at most 0.0033.
Values may be sent and summed in bfloat16 or wider, within the bound.
No kernel may reach another device: no remote copies, remote signals or barrier semaphores. Data moves between devices by JAX's collectives and lax.ppermute only.
A program may use at most 64 MiB of HBM per device.

v0:
```python
import functools
import math
import jax
import jax.numpy as jnp
from jax import lax
from jax.sharding import Mesh
from jax.sharding import PartitionSpec as P

GRID_MERIDIANS = 1440
HARMONIC_ORDERS = 720
LAT_LEV = ("lat", "lev_0", "lev_1", "lev_2")
epsilon = 1e-06


def from_everyone(array, axis):
    copies = jnp.broadcast_to(array, (lax.axis_size(axis), *array.shape))
    return lax.all_to_all(copies, axis, split_axis=0, concat_axis=0, tiled=True)


def over_copies(array, axis):
    everything = from_everyone(array, axis)
    return jnp.sum(everything, axis=0)


def in_one(arrays, axis):
    flat, at, outs = (jnp.concatenate([a.reshape(-1) for a in arrays]), 0, [])
    so_far = over_copies(flat, axis)
    for a in arrays:
        outs.append(so_far[at : at + a.size].reshape(a.shape))
        at += a.size
    return tuple(outs)


def nothing_yet(array, identity):
    return jnp.broadcast_to(jnp.asarray(identity, array.dtype), array.shape)


def prefix_by_axis(array, axes, combine, identity):
    before = start = nothing_yet(array, identity)
    so_far = array
    for axis in reversed(axes):
        length, place = (lax.axis_size(axis), lax.axis_index(axis))
        pieces = lax.all_gather(so_far, axis)
        inside, so_far = (start, start)
        for k in range(length):
            passed = k < place
            so_far = combine(so_far, pieces[k])
            inside = jnp.where(passed, so_far, inside)
        before = combine(inside, before)
    return before


def one_axis_at_a_time(array, axes):
    return functools.reduce(lax.pmax, axes, array)


def over_axes(array, axes):
    for axis in axes:
        array = lax.psum(array, axis)
    return array


def build_waves(wave_rows, lon_index):
    wavenumber = wave_rows // 2 + 1
    component = wave_rows % 2
    turns = wavenumber[:, None] * lon_index[None, :] % GRID_MERIDIANS
    angle = turns.astype(jnp.float32) * (2.0 * math.pi / GRID_MERIDIANS)
    return jnp.where(component[:, None] == 0, jnp.cos(angle), jnp.sin(angle)).astype(jnp.bfloat16)


def add_arrays(earlier, later):
    return earlier + later


def cospectra(fourier_weights, norm_factor):
    heat_part = norm_factor * (
        fourier_weights[:, 0, 1] * fourier_weights[:, 0, 2]
        + fourier_weights[:, 1, 1] * fourier_weights[:, 1, 2]
    )
    moment_part = norm_factor * (
        fourier_weights[:, 0, 0] * fourier_weights[:, 0, 1]
        + fourier_weights[:, 1, 0] * fourier_weights[:, 1, 1]
    )
    return (heat_part, moment_part)


def per_device(
    along_axis_flow,
    poleward_flow,
    warmth_departure,
    validity_indicator,
    layer_depth_span,
    desired_circulation_norm,
):
    bands, batch, level_values, lon_count = poleward_flow.shape
    lon_ways = lax.axis_size("lon")
    retained_indicator = validity_indicator.astype(jnp.bfloat16)[:, None]
    screened_eastward_speed = along_axis_flow * retained_indicator
    screened_northward_speed = poleward_flow * retained_indicator
    screened_thermal_anomaly = warmth_departure * retained_indicator
    zonal_v = jnp.sum(screened_northward_speed, axis=3, dtype=jnp.float32)
    kept_count = jnp.sum(validity_indicator, axis=2).astype(jnp.float32)
    zonal_v, kept_count = in_one((zonal_v, kept_count), "lon")
    mean_v = zonal_v / jnp.maximum(kept_count, 1.0)[:, None, :]
    columns = batch * level_values
    joined_arrays = jnp.stack(
        [screened_eastward_speed, screened_northward_speed, screened_thermal_anomaly]
    ).reshape(3, bands, columns, lon_count)
    norm_factor = 2.0 / (GRID_MERIDIANS * GRID_MERIDIANS)
    wave_local = HARMONIC_ORDERS // lon_ways
    own_rows = lax.axis_index("lon") * (2 * wave_local) + jnp.arange(
        2 * wave_local, dtype=jnp.int32
    )
    waves_table = build_waves(own_rows, jnp.arange(GRID_MERIDIANS, dtype=jnp.int32))
    fourier_weights = lax.dot_general(
        waves_table,
        lax.all_gather(joined_arrays, "lon", axis=3, tiled=True),
        (((1,), (3,)), ((), ())),
        preferred_element_type=jnp.float32,
    )
    fourier_weights = fourier_weights.reshape(wave_local, 2, 3, bands, columns)
    heat_cospec, momentum_cospec = cospectra(fourier_weights, norm_factor)
    nlat = bands * lax.axis_size(LAT_LEV)
    band_index = lax.axis_index(LAT_LEV) * bands + jnp.arange(bands, dtype=jnp.int32)
    latitude = ((band_index.astype(jnp.float32) + 0.5) / nlat - 0.5) * math.pi
    cosine = jnp.cos(latitude)
    weighted = mean_v * cosine[:, None, None] * layer_depth_span[None, None, :]
    upward = jnp.cumsum(weighted, axis=2)
    southward = jnp.cumsum(upward, axis=0)
    band_sums = southward[-1]
    southern = prefix_by_axis(
        band_sums, LAT_LEV, add_arrays, jnp.zeros((batch, level_values), jnp.float32)
    )
    stream = southward + southern[None]
    local_peak = jnp.max(jnp.abs(stream))
    cell_count = batch * level_values * nlat
    weight_lat = cosine[:, None, None]
    peak_value = one_axis_at_a_time(local_peak, LAT_LEV)
    psi_norm = stream / (peak_value + epsilon)
    local_misfit = jnp.sum(weight_lat * (psi_norm - desired_circulation_norm) ** 2)
    budget_penalty = over_axes(local_misfit, LAT_LEV) / cell_count
    return (psi_norm, heat_cospec, momentum_cospec, budget_penalty)


def solution(mesh):
    torus = Mesh(
        mesh.devices.reshape(mesh.shape["lat"], mesh.shape["lon"], 8, 4, 2),
        ("lat", "lon", "lev_0", "lev_1", "lev_2"),
    )
    in_specs = (
        P(LAT_LEV, None, None, "lon"),
        P(LAT_LEV, None, None, "lon"),
        P(LAT_LEV, None, None, "lon"),
        P(LAT_LEV, None, "lon"),
        P(),
        P(LAT_LEV, None, None),
    )
    out_specs = (P(LAT_LEV, None, None), P("lon", LAT_LEV, None), P("lon", LAT_LEV, None), P())
    return jax.shard_map(
        per_device, mesh=torus, in_specs=in_specs, out_specs=out_specs, check_vma=False
    )
```

profile of v0, /device:TPU:1, one launch (start us, length us, event | category | flops | bytes accessed | tf_op | source)
XLA Modules:
  0.0 185.7 jit_solution(17721754598539388875)
XLA Ops:
  7.2 1.4 fusion.27
  8.6 1.5 convert_reduce_fusion
  10.2 0.8 copy.48
  11.0 1.6 broadcast_multiply_fusion.1
  12.6 1.3 copy.47
  13.9 0.8 copy.49
  14.8 3.0 %pad_maximum_fusion = bf16[3,5,128,720]{2,3,1,0:T(8,128)(2,1)} fusion(bf16[1,5,128,720]{2,3,1,0:T(8,128)(2,1)S(1)} %copy.49, bf16[1,5,128,720]{2,3,1,0:T(8,128)(2,1)S(1)} %copy.48, bf16[1,5,128,720]{2,3,1,0:T(8,128)(2,1)} %copy.47), kind=kLoop, calls=%fused_computation.8 | loop fusion | flops 2764800 | bytes 5529600 | tf_op jit(solution)/shard_map/stack | solution.py:106
  17.8 0.1 convert_element_type.29
  17.9 0.1 reshape.104
  18.0 0.6 broadcast_in_dim.9
  18.6 3.3 %all-to-all-start = ((f32[2,1,800]{2,1,0:T(1,128)}), f32[2,1,800]{2,1,0:T(1,128)S(1)}, u32[]{:S(2)}, u32[]{:S(2)}) async-start(f32[2,1,800]{2,1,0:T(1,128)} %broadcast_in_dim.9), calls=%async_computation | async-start | bytes 14336 | tf_op jit(solution)/shard_map/all_to_all | solution.py:17
  22.0 3.1 %all-to-all-done = f32[2,1,800]{2,1,0:T(1,128)S(1)} async-done(((f32[2,1,800]{2,1,0:T(1,128)}), f32[2,1,800]{2,1,0:T(1,128)S(1)}, u32[]{:S(2)}, u32[]{:S(2)}) %all-to-all-start) | async-done | bytes 6432 | tf_op jit(solution)/shard_map/all_to_all | solution.py:17
  25.1 0.1 max.23
  25.1 0.1 reshape.105
  25.3 1.0 reduce_window_sum.22
  26.3 5.3 %all_gather.18 = f32[2,4,32]{2,1,0:T(4,128)S(1)} all-gather(f32[1,4,32]{2,1,0:T(4,128)S(1)} %slice.110), channel_id=1, replica_groups=mesh['lat'=2,'lon'=2,'lev_0'=8,'lev_1'=4,'lev_2'=2] {'lev_2'}, dimensions={0}, use_global_device_ids=true | all-gather | bytes 1536 | tf_op jit(solution)/shard_map/all_gather | solution.py:43
  31.6 8.1 %all_gather.19 = f32[4,4,32]{2,1,0:T(4,128)S(1)} all-gather(f32[1,4,32]{2,1,0:T(4,128)S(1)} %slice_add_fusion.11), channel_id=1, replica_groups=mesh['lat'=2,'lon'=2,'lev_0'=8,'lev_1'=4,'lev_2'=2] {'lev_1'}, dimensions={0}, use_global_device_ids=true | all-gather | bytes 2560 | tf_op jit(solution)/shard_map/all_gather | solution.py:43
  39.7 20.2 %all_gather.20 = f32[8,4,32]{2,1,0:T(4,128)S(1)} all-gather(f32[1,4,32]{2,1,0:T(4,128)S(1)} %slice_add_fusion.8), channel_id=1, replica_groups=mesh['lat'=2,'lon'=2,'lev_0'=8,'lev_1'=4,'lev_2'=2] {'lev_0'}, dimensions={0}, use_global_device_ids=true | all-gather | bytes 4608 | tf_op jit(solution)/shard_map/all_gather | solution.py:43
  59.9 4.9 %all_gather.21 = f32[2,4,32]{2,1,0:T(4,128)S(1)} all-gather(f32[1,4,32]{2,1,0:T(4,128)S(1)} %get-tuple-element.6), channel_id=1, replica_groups=mesh['lat'=2,'lon'=2,'lev_0'=8,'lev_1'=4,'lev_2'=2] {'lat'}, dimensions={0}, use_global_device_ids=true | all-gather | bytes 1536 | tf_op jit(solution)/shard_map/all_gather | solution.py:43
  64.8 0.6 abs_reduce_fusion
  65.5 6.1 %pmax.28 = f32[]{:T(128)} all-reduce(f32[]{:T(128)} %abs_reduce_fusion), channel_id=1, replica_groups=mesh['lat'=2,'lon'=2,'lev_0'=8,'lev_1'=4,'lev_2'=2] {'lat'}, use_global_device_ids=true, to_apply=%region_6.7 | all-reduce | flops 1 | bytes 8 | tf_op jit(solution)/shard_map/pmax | solution.py:54
  71.6 12.4 %pmax.29 = f32[]{:T(128)} all-reduce(f32[]{:T(128)} %pmax.28), channel_id=1, replica_groups=mesh['lat'=2,'lon'=2,'lev_0'=8,'lev_1'=4,'lev_2'=2] {'lev_0'}, use_global_device_ids=true, to_apply=%region_7.8 | all-reduce | flops 1 | bytes 8 | tf_op jit(solution)/shard_map/pmax | solution.py:54
  83.9 8.3 %pmax.30 = f32[]{:T(128)} all-reduce(f32[]{:T(128)} %pmax.29), channel_id=1, replica_groups=mesh['lat'=2,'lon'=2,'lev_0'=8,'lev_1'=4,'lev_2'=2] {'lev_1'}, use_global_device_ids=true, to_apply=%region_8.9 | all-reduce | flops 1 | bytes 8 | tf_op jit(solution)/shard_map/pmax | solution.py:54
  92.2 17.9 %pmax.31 = f32[]{:T(128)} all-reduce(f32[]{:T(128)} %pmax.30), channel_id=1, replica_groups=mesh['lat'=2,'lon'=2,'lev_0'=8,'lev_1'=4,'lev_2'=2] {'lev_2'}, use_global_device_ids=true, to_apply=%region_9.10 | all-reduce | flops 1 | bytes 8 | tf_op jit(solution)/shard_map/pmax | solution.py:54
  110.7 1.2 multiply_reduce_fusion
  111.9 5.9 %psum.28 = f32[]{:T(128)} all-reduce(f32[]{:T(128)} %get-tuple-element.4), channel_id=1, replica_groups=mesh['lat'=2,'lon'=2,'lev_0'=8,'lev_1'=4,'lev_2'=2] {'lat'}, use_global_device_ids=true, to_apply=%region_11.12 | all-reduce | flops 1 | bytes 8 | tf_op jit(solution)/shard_map/psum | solution.py:59
  117.8 11.7 %psum.29 = f32[]{:T(128)} all-reduce(f32[]{:T(128)} %psum.28), channel_id=1, replica_groups=mesh['lat'=2,'lon'=2,'lev_0'=8,'lev_1'=4,'lev_2'=2] {'lev_0'}, use_global_device_ids=true, to_apply=%region_12.13 | all-reduce | flops 1 | bytes 8 | tf_op jit(solution)/shard_map/psum | solution.py:59
  129.6 6.6 %psum.30 = f32[]{:T(128)} all-reduce(f32[]{:T(128)} %psum.29), channel_id=1, replica_groups=mesh['lat'=2,'lon'=2,'lev_0'=8,'lev_1'=4,'lev_2'=2] {'lev_1'}, use_global_device_ids=true, to_apply=%region_13.14 | all-reduce | flops 1 | bytes 8 | tf_op jit(solution)/shard_map/psum | solution.py:59
  136.2 10.1 %psum.31 = f32[]{:T(128)} all-reduce(f32[]{:T(128)} %psum.30), channel_id=1, replica_groups=mesh['lat'=2,'lon'=2,'lev_0'=8,'lev_1'=4,'lev_2'=2] {'lev_2'}, use_global_device_ids=true, to_apply=%region_14.15 | all-reduce | flops 1 | bytes 8 | tf_op jit(solution)/shard_map/psum | solution.py:59
  147.0 25.1 %fusion.6 = f32[720,3,5,128]{3,0,2,1:T(8,128)S(1)} fusion(bf16[3,5,128,1440]{2,3,1,0:T(8,128)(2,1)} %all-gather.2.cloned.1.call-done, s32[720]{0:T(1024)S(1)} %fusion.14, pred[720]{0:T(1024)(128)(4,1)S(1)} %fusion.13), kind=kOutput, calls=%fused_computation.10 | convolution fusion | flops 3992716800 | bytes 11062800 | tf_op jit(solution)/shard_map/dot_general | solution.py:115
  172.1 3.9 %fusion.26 = (f32[360,1,1,5,128]{4,1,0,3,2:T(1,128)S(1)}, f32[360,1,1,5,128]{4,1,0,3,2:T(1,128)S(1)}, f32[360,1,1,5,128]{4,1,0,3,2:T(1,128)S(1)}, f32[360,1,1,5,...) fusion(f32[360,2,3,5,128]{4,1,0,3,2:T(2,128)S(1)} %bitcast.27), kind=kLoop, calls=%fused_computation.61 | loop fusion | bytes 11059200 | tf_op jit(solution)/shard_map/slice | solution.py:81
  176.0 1.7 multiply_bitcast_fusion
  (21 shorter events, 0.3 us)
Async XLA Ops:
  7.2 139.8 %all-gather.2.cloned.1.call-start = ((), (), s32[]{:S(2)}) async-start(), calls=%async_computation.1 | async-start | bytes 8294400 | tf_op jit(solution)/shard_map/all_gather | solution.py:117
  14.7 10.5 %copy-start.1 = (f32[32]{0:T(128)S(1)}, f32[32]{0:T(128)}, u32[]{:S(2)}) copy-start(f32[32]{0:T(128)} %param.10) | copy-start | bytes 388
  14.8 96.0 %copy-start = (f32[5,4,32]{2,1,0:T(4,128)S(1)}, f32[5,4,32]{2,1,0:T(4,128)}, u32[]{:S(2)}) copy-start(f32[5,4,32]{2,1,0:T(4,128)} %param.11) | copy-start | bytes 7684
  18.6 6.4 %all-to-all-start = ((f32[2,1,800]{2,1,0:T(1,128)}), f32[2,1,800]{2,1,0:T(1,128)S(1)}, u32[]{:S(2)}, u32[]{:S(2)}) async-start(f32[2,1,800]{2,1,0:T(1,128)} %broadcast_in_dim.9), calls=%async_computation | async-start | bytes 14336 | tf_op jit(solution)/shard_map/all_to_all | solution.py:17
Sparse Core Ops, SparseCore 0:
  17.9 80.5 all-gather.1
where the time goes:
time: 186 us
  blocking collectives  117 us (63%)
  matrix products  25.1 us (13%)
  between operations  16.6 us (9%)
  other arithmetic  12.4 us (7%)
  local copies, waits for them, and re-layouts  7.7 us (4%)
  starting transfers between devices  3.33 us (2%)
  waiting for transfers between devices  3.1 us (2%)
    pmax x4, blocking collectives, one_axis_at_a_time(): return functools.reduce(lax.pmax, axes, array)  44.6 us
    all_gather x4, blocking collectives, prefix_by_axis(): pieces = lax.all_gather(so_far, axis)  38.5 us
    psum x4, blocking collectives, over_axes(): array = lax.psum(array, axis)  34.3 us
    dot_general x1, matrix products, per_device(): lax.dot_general(waves_table, lax.all_gather(joined_arrays, 'lon', axis=3,...  25.1 us
    slice x1, local copies, waits for them, and re-layouts, cospectra(): fourier_weights[:, 0, 0] * fourier_weights[:, 0, 1]  3.85 us
  transfers between devices with their start and end apart: 2, of which 1 were waited for; matrix products, arithmetic and copies ran while one was open for 2% of the time, Pallas kernels for 0%

commit v1 on v0

--- a/solution.py
+++ b/solution.py
@@ -56,7 +56,7 @@
 
 def over_axes(array, axes):
     for axis in axes:
-        array = lax.psum(array, axis)
+        array = jnp.sum(lax.all_gather(array, axis), axis=0)
     return array
 
 

time: 186 us -> 194 us (1.043)
  local copies, waits for them, and re-layouts: 7.7 us -> 15.7 us
  other arithmetic: 12.4 us -> 14.8 us
  blocking collectives: 117 us -> 115 us
    psum x4 -> x0, blocking collectives: 34.3 us -> none  [over_axes(): array = lax.psum(array, axis)]
    unnamed x0 -> x4, blocking collectives: none -> 31.7 us
    unnamed x4 -> x24, local copies, waits for them, and re-layouts: 0.01 us -> 7.98 us
    reduce_sum x0 -> x4, other arithmetic: none -> 2.41 us  [over_axes(): array = jnp.sum(lax.all_gather(array, axis), axis=0)]
  transfers between devices with their start and end apart: 2 -> 2, of which waited for: 1 -> 1; matrix products, arithmetic and copies ran while one was open for 2% -> 7% of each run, Pallas kernels for 0% -> 0%
where the time goes in v1:
time: 194 us; the launch traced here: 193 us
  blocking collectives  115 us (59%)
  matrix products  25.1 us (13%)
  between operations  16.7 us (9%)
  local copies, waits for them, and re-layouts  15.7 us (8%)
  other arithmetic  14.8 us (8%)
  starting transfers between devices  3.33 us (2%)
  waiting for transfers between devices  3.06 us (2%)
    pmax x4, blocking collectives, one_axis_at_a_time(): return functools.reduce(lax.pmax, axes, array)  44.6 us
    all_gather x4, blocking collectives, prefix_by_axis(): pieces = lax.all_gather(so_far, axis)  38.5 us
    unnamed x4, blocking collectives  31.7 us
    dot_general x1, matrix products, per_device(): lax.dot_general(waves_table, lax.all_gather(joined_arrays, 'lon', axis=3,...  25.1 us
    unnamed x24, local copies, waits for them, and re-layouts  7.98 us
  transfers between devices with their start and end apart: 2, of which 1 were waited for; matrix products, arithmetic and copies ran while one was open for 7% of the time, Pallas kernels for 0%

profile of v1, /device:TPU:1, one launch (start us, length us, event | category | flops | bytes accessed | tf_op | source)
XLA Modules:
  0.0 193.5 jit_solution(1340519370722633851)
XLA Ops:
  7.2 1.4 fusion.27
  8.6 1.5 convert_reduce_fusion
  10.2 0.8 copy.48
  11.0 1.6 broadcast_multiply_fusion.1
  12.6 1.3 copy.47
  13.9 0.8 copy.49
  14.8 3.0 %pad_maximum_fusion = bf16[3,5,128,720]{2,3,1,0:T(8,128)(2,1)} fusion(bf16[1,5,128,720]{2,3,1,0:T(8,128)(2,1)S(1)} %copy.49, bf16[1,5,128,720]{2,3,1,0:T(8,128)(2,1)S(1)} %copy.48, bf16[1,5,128,720]{2,3,1,0:T(8,128)(2,1)} %copy.47), kind=kLoop, calls=%fused_computation.8 | loop fusion | flops 2764800 | bytes 5529600 | tf_op jit(solution)/shard_map/stack | solution.py:106
  18.1 0.6 broadcast_in_dim.9
  18.7 3.3 %all-to-all-start = ((f32[2,1,800]{2,1,0:T(1,128)}), f32[2,1,800]{2,1,0:T(1,128)S(1)}, u32[]{:S(2)}, u32[]{:S(2)}) async-start(f32[2,1,800]{2,1,0:T(1,128)} %broadcast_in_dim.9), calls=%async_computation | async-start | bytes 14336 | tf_op jit(solution)/shard_map/all_to_all | solution.py:17
  22.1 3.0 %all-to-all-done = f32[2,1,800]{2,1,0:T(1,128)S(1)} async-done(((f32[2,1,800]{2,1,0:T(1,128)}), f32[2,1,800]{2,1,0:T(1,128)S(1)}, u32[]{:S(2)}, u32[]{:S(2)}) %all-to-all-start) | async-done | bytes 6432 | tf_op jit(solution)/shard_map/all_to_all | solution.py:17
  25.4 1.0 reduce_window_sum.22
  26.4 5.3 %all_gather.42 = f32[2,4,32]{2,1,0:T(4,128)S(1)} all-gather(f32[1,4,32]{2,1,0:T(4,128)S(1)} %slice.110), channel_id=1, replica_groups=mesh['lat'=2,'lon'=2,'lev_0'=8,'lev_1'=4,'lev_2'=2] {'lev_2'}, dimensions={0}, use_global_device_ids=true | all-gather | bytes 1536 | tf_op jit(solution)/shard_map/all_gather | solution.py:43
  31.7 8.1 %all_gather.43 = f32[4,4,32]{2,1,0:T(4,128)S(1)} all-gather(f32[1,4,32]{2,1,0:T(4,128)S(1)} %slice_add_fusion.11), channel_id=1, replica_groups=mesh['lat'=2,'lon'=2,'lev_0'=8,'lev_1'=4,'lev_2'=2] {'lev_1'}, dimensions={0}, use_global_device_ids=true | all-gather | bytes 2560 | tf_op jit(solution)/shard_map/all_gather | solution.py:43
  39.8 20.2 %all_gather.44 = f32[8,4,32]{2,1,0:T(4,128)S(1)} all-gather(f32[1,4,32]{2,1,0:T(4,128)S(1)} %slice_add_fusion.8), channel_id=1, replica_groups=mesh['lat'=2,'lon'=2,'lev_0'=8,'lev_1'=4,'lev_2'=2] {'lev_0'}, dimensions={0}, use_global_device_ids=true | all-gather | bytes 4608 | tf_op jit(solution)/shard_map/all_gather | solution.py:43
  60.0 4.9 %all_gather.45 = f32[2,4,32]{2,1,0:T(4,128)S(1)} all-gather(f32[1,4,32]{2,1,0:T(4,128)S(1)} %get-tuple-element.6), channel_id=1, replica_groups=mesh['lat'=2,'lon'=2,'lev_0'=8,'lev_1'=4,'lev_2'=2] {'lat'}, dimensions={0}, use_global_device_ids=true | all-gather | bytes 1536 | tf_op jit(solution)/shard_map/all_gather | solution.py:43
  64.9 0.6 abs_reduce_fusion
  65.5 6.1 %pmax.28 = f32[]{:T(128)} all-reduce(f32[]{:T(128)} %abs_reduce_fusion), channel_id=1, replica_groups=mesh['lat'=2,'lon'=2,'lev_0'=8,'lev_1'=4,'lev_2'=2] {'lat'}, use_global_device_ids=true, to_apply=%region_6.7 | all-reduce | flops 1 | bytes 8 | tf_op jit(solution)/shard_map/pmax | solution.py:54
  71.6 12.4 %pmax.29 = f32[]{:T(128)} all-reduce(f32[]{:T(128)} %pmax.28), channel_id=1, replica_groups=mesh['lat'=2,'lon'=2,'lev_0'=8,'lev_1'=4,'lev_2'=2] {'lev_0'}, use_global_device_ids=true, to_apply=%region_7.8 | all-reduce | flops 1 | bytes 8 | tf_op jit(solution)/shard_map/pmax | solution.py:54
  84.0 8.3 %pmax.30 = f32[]{:T(128)} all-reduce(f32[]{:T(128)} %pmax.29), channel_id=1, replica_groups=mesh['lat'=2,'lon'=2,'lev_0'=8,'lev_1'=4,'lev_2'=2] {'lev_1'}, use_global_device_ids=true, to_apply=%region_8.9 | all-reduce | flops 1 | bytes 8 | tf_op jit(solution)/shard_map/pmax | solution.py:54
  92.9 17.9 %pmax.31 = f32[]{:T(128)} all-reduce(f32[]{:T(128)} %pmax.30), channel_id=1, replica_groups=mesh['lat'=2,'lon'=2,'lev_0'=8,'lev_1'=4,'lev_2'=2] {'lev_2'}, use_global_device_ids=true, to_apply=%region_9.10 | all-reduce | flops 1 | bytes 8 | tf_op jit(solution)/shard_map/pmax | solution.py:54
  111.4 1.2 multiply_reduce_fusion
  112.6 1.4 dynamic-update-slice
  114.6 5.3 %all-reduce = f32[2]{0:T(128)S(1)} all-reduce(f32[2]{0:T(128)S(1)} %dynamic-update-slice), channel_id=1, replica_groups=mesh['lat'=2,'lon'=2,'lev_0'=8,'lev_1'=4,'lev_2'=2] {'lat'}, use_global_device_ids=true, to_apply=%add | all-reduce | flops 2 | bytes 16
  120.5 1.4 dynamic-update-slice.1
  122.4 11.1 %all-reduce.1 = f32[8]{0:T(128)S(1)} all-reduce(f32[8]{0:T(128)S(1)} %dynamic-update-slice.1), channel_id=1, replica_groups=mesh['lat'=2,'lon'=2,'lev_0'=8,'lev_1'=4,'lev_2'=2] {'lev_0'}, use_global_device_ids=true, to_apply=%add.1 | all-reduce | flops 8 | bytes 64
  134.1 1.4 dynamic-update-slice.2
  136.1 6.0 %all-reduce.2 = f32[4]{0:T(128)S(1)} all-reduce(f32[4]{0:T(128)S(1)} %dynamic-update-slice.2), channel_id=1, replica_groups=mesh['lat'=2,'lon'=2,'lev_0'=8,'lev_1'=4,'lev_2'=2] {'lev_1'}, use_global_device_ids=true, to_apply=%add.2 | all-reduce | flops 4 | bytes 32
  142.7 1.4 dynamic-update-slice.3
  144.1 9.4 %all-reduce.3 = f32[2]{0:T(128)S(1)} all-reduce(f32[2]{0:T(128)S(1)} %dynamic-update-slice.3), channel_id=1, replica_groups=mesh['lat'=2,'lon'=2,'lev_0'=8,'lev_1'=4,'lev_2'=2] {'lev_2'}, use_global_device_ids=true, to_apply=%add.3 | all-reduce | flops 2 | bytes 16
  154.8 25.1 %fusion.6 = f32[720,3,5,128]{3,0,2,1:T(8,128)S(1)} fusion(bf16[3,5,128,1440]{2,3,1,0:T(8,128)(2,1)} %all-gather.2.cloned.1.call-done, s32[720]{0:T(1024)S(1)} %fusion.14, pred[720]{0:T(1024)(128)(4,1)S(1)} %fusion.13), kind=kOutput, calls=%fused_computation.10 | convolution fusion | flops 3992716800 | bytes 11062800 | tf_op jit(solution)/shard_map/dot_general | solution.py:115
  179.9 3.9 %fusion.26 = (f32[360,1,1,5,128]{4,1,0,3,2:T(1,128)S(1)}, f32[360,1,1,5,128]{4,1,0,3,2:T(1,128)S(1)}, f32[360,1,1,5,128]{4,1,0,3,2:T(1,128)S(1)}, f32[360,1,1,5,...) fusion(f32[360,2,3,5,128]{4,1,0,3,2:T(2,128)S(1)} %bitcast.35), kind=kLoop, calls=%fused_computation.61 | loop fusion | bytes 11059200 | tf_op jit(solution)/shard_map/slice | solution.py:81
  183.8 1.7 multiply_bitcast_fusion
  (45 shorter events, 5.4 us)
Async XLA Ops:
  7.2 147.6 %all-gather.2.cloned.1.call-start = ((), (), s32[]{:S(2)}) async-start(), calls=%async_computation.1 | async-start | bytes 8294400 | tf_op jit(solution)/shard_map/all_gather | solution.py:117
  14.7 10.5 %copy-start.1 = (f32[32]{0:T(128)S(1)}, f32[32]{0:T(128)}, u32[]{:S(2)}) copy-start(f32[32]{0:T(128)} %param.10) | copy-start | bytes 388
  14.8 77.5 %copy-start.5 = (u32[256]{0:T(256)S(1)}, u32[256]{0:T(256)}, u32[]{:S(2)}) copy-start(u32[256]{0:T(256)} %constant.114) | copy-start | bytes 3076
  14.8 96.6 %copy-start = (f32[5,4,32]{2,1,0:T(4,128)S(1)}, f32[5,4,32]{2,1,0:T(4,128)}, u32[]{:S(2)}) copy-start(f32[5,4,32]{2,1,0:T(4,128)} %param.11) | copy-start | bytes 7684
  14.8 99.2 %copy-start.4 = (u32[256]{0:T(256)S(1)}, u32[256]{0:T(256)}, u32[]{:S(2)}) copy-start(u32[256]{0:T(256)} %constant.119) | copy-start | bytes 3076
  14.8 107.1 %copy-start.3 = (u32[256]{0:T(256)S(1)}, u32[256]{0:T(256)}, u32[]{:S(2)}) copy-start(u32[256]{0:T(256)} %constant.124) | copy-start | bytes 3076
  14.8 120.7 %copy-start.2 = (u32[256]{0:T(256)S(1)}, u32[256]{0:T(256)}, u32[]{:S(2)}) copy-start(u32[256]{0:T(256)} %constant.129) | copy-start | bytes 3076
  18.7 6.4 %all-to-all-start = ((f32[2,1,800]{2,1,0:T(1,128)}), f32[2,1,800]{2,1,0:T(1,128)S(1)}, u32[]{:S(2)}, u32[]{:S(2)}) async-start(f32[2,1,800]{2,1,0:T(1,128)} %broadcast_in_dim.9), calls=%async_computation | async-start | bytes 14336 | tf_op jit(solution)/shard_map/all_to_all | solution.py:17
Sparse Core Ops, SparseCore 0:
  18.0 80.5 all-gather.1
